TPU v7x, 32 devices: a whole 2x2x4 slice. The times are simulated.
32 devices in a mesh: row: 4 (over z), col: 2 (over y), depth: 4 (over x, core).
Axes of the slice: x: 2, y: 2, z: 4, core: 2. Of those that a mesh axis runs over, the one named last changes fastest.
Arguments:
- a21_leaf: float32 [4, 4096, 2048], P('depth', 'row', 'col'), may hold values from -1.2 to 1.2
- a12_leaf: float32 [4, 2048, 4096], P('depth', 'row', 'col'), may hold values from -1.2 to 1.2
- uinv_leaf: float32 [4, 2048, 2048], P('depth', None, 'col'), may hold values from -0.2 to 1.5, as said below
- linv_leaf: float32 [4, 2048, 2048], P('depth', 'row'), may hold values from -0.2 to 1.5, as said below
- live: int32 [4], P('depth'), may hold values from 16 to 32
- row_map: int32 [4, 32], P('depth', 'row'), may hold values from 0 to 63, as said below
- col_map: int32 [4, 32], P('depth', 'col'), may hold values from 0 to 63, as said below
- a22_anc: float32 [8192, 8192], P(('row', 'depth'), 'col'), may hold values from -6 to 6
- a21_anc: float32 [8192, 2048], P(('row', 'depth'), 'col'), may hold values from -1.2 to 1.2
- a12_anc: float32 [2048, 8192], P(('row', 'depth'), 'col'), may hold values from -1.2 to 1.2
- uinv_anc: float32 [2048, 2048], P(None, 'col'), may hold values from -0.2 to 1.5, as said below
- linv_anc: float32 [2048, 2048], P(('row', 'depth')), may hold values from -0.2 to 1.5, as said below
Outputs:
- leaf_lower: float32 [4, 4096, 2048], P('depth', 'row', 'col')
- leaf_upper: float32 [4, 2048, 4096], P('depth', 'row', 'col')
- anc_lower: float32 [8192, 2048], P(('row', 'depth'), 'col')
- anc_upper: float32 [2048, 8192], P(('row', 'depth'), 'col')
- anc_schur: float32 [8192, 8192], P(('row', 'depth'), 'col')
Inputs may be any that keep to these rules, and one draw needn't show every extreme that they name: `uinv_leaf`: upper triangular: zero below the diagonal, diagonal between 0.5 and 1.5. `linv_leaf`: lower triangular: zero above the diagonal, diagonal between 0.5 and 1.5. `uinv_anc`: upper triangular: zero below the diagonal, diagonal between 0.5 and 1.5. `linv_anc`: lower triangular: zero above the diagonal, diagonal between 0.5 and 1.5. `row_map`: within one replica the entries are distinct. Leaf block row i lies in the k-th of 4 equal ranges of leaf block rows, and its target lies in the k-th of 4 equal ranges of the 64 ancestor block rows. `col_map`: within one replica the entries are distinct. Leaf block column j lies in the k-th of 2 equal ranges of leaf block columns, and its target lies in the k-th of 2 equal ranges of the 64 ancestor block columns.
All inputs are finite; a program needn't handle non-finite values.
Results may differ from a plain program's by a relative error of at most 0.0001.
Values sent between devices are 32-bit elements; how exact they have to be, the bound alone decides.
A program may use at most 256 MiB of HBM per device.

v0:
```python
import jax
import jax.numpy as jnp
from jax import lax
from jax.sharding import PartitionSpec as P

NB = 128


def product(left, right):
    return jnp.dot(left, right, precision=lax.Precision.HIGHEST, preferred_element_type=jnp.float32)


def reduce_depth(update):
    return lax.psum_scatter(update, "depth", scatter_dimension=0, tiled=True)


def combine_depth(schur, row_map, col_map, a22_anc):
    block_size = NB
    rows_here = schur.shape[0]
    cols_here = schur.shape[1]
    leaf_rows = rows_here // block_size
    leaf_cols = cols_here // block_size
    anc_rows = a22_anc.shape[0]
    replicas = lax.axis_size("depth")
    anc_row_blocks = anc_rows * replicas // block_size
    anc_col_blocks = a22_anc.shape[1] // block_size
    row_local = row_map[0] - lax.axis_index("row") * anc_row_blocks
    col_local = col_map[0] - lax.axis_index("col") * anc_col_blocks
    col_pick = (col_local[:, None] == lax.iota(jnp.int32, anc_col_blocks)[None, :]).astype(
        jnp.float32
    )
    row_pick = (row_local[:, None] == lax.iota(jnp.int32, anc_row_blocks)[None, :]).astype(
        jnp.float32
    )
    leaf_blocks = schur.reshape(leaf_rows, block_size, leaf_cols, block_size)
    placed = jnp.einsum("ia,ixjy->axjy", row_pick, leaf_blocks, precision=lax.Precision.HIGHEST)
    placed = jnp.einsum("axjy,jb->axby", placed, col_pick, precision=lax.Precision.HIGHEST)
    update = placed.reshape(anc_row_blocks * block_size, anc_col_blocks * block_size)
    return reduce_depth(update)


def anc_panels(a21_anc, a12_anc, uinv_anc, linv_anc):
    factor = uinv_anc
    anc_lower = product(lax.all_gather(a21_anc, "col", axis=1, tiled=True), factor)
    lower_whole = lax.all_gather(anc_lower, "col", axis=1, tiled=True)
    factor = linv_anc
    anc_upper = product(factor, lax.all_gather(a12_anc, ("row", "depth"), axis=0, tiled=True))
    return (anc_lower, lower_whole, anc_upper)


def shards(
    a21_leaf,
    a12_leaf,
    uinv_leaf,
    linv_leaf,
    live,
    row_map,
    col_map,
    a22_anc,
    a21_anc,
    a12_anc,
    uinv_anc,
    linv_anc,
):
    block_size = NB
    panel_left = a21_leaf[0]
    panel_top = a12_leaf[0]
    upper_inverse = uinv_leaf[0]
    lower_inverse = linv_leaf[0]
    rows_here = panel_left.shape[0]
    cols_here = panel_top.shape[1]
    live_rows = live[0] * block_size
    row_pos = lax.axis_index("row") * rows_here + lax.iota(jnp.int32, rows_here)
    col_pos = lax.axis_index("col") * cols_here + lax.iota(jnp.int32, cols_here)
    row_keep = (row_pos < live_rows).astype(jnp.float32)
    col_keep = (col_pos < live_rows).astype(jnp.float32)
    factor = upper_inverse
    lower_part = product(lax.all_gather(panel_left, "col", axis=1, tiled=True), factor)
    leaf_lower = lower_part * row_keep[:, None]
    factor = lower_inverse
    upper_part = product(factor, lax.all_gather(panel_top, "row", axis=0, tiled=True))
    leaf_upper = upper_part * col_keep[None, :]
    upper_whole = lax.all_gather(leaf_upper, "row", axis=0, tiled=True)
    factor = upper_whole
    schur = jnp.zeros((rows_here, cols_here), jnp.float32) - product(
        lax.all_gather(leaf_lower, "col", axis=1, tiled=True), factor
    )
    own_update = combine_depth(schur, row_map, col_map, a22_anc)
    anc_lower, lower_whole, anc_upper = anc_panels(a21_anc, a12_anc, uinv_anc, linv_anc)
    factor = lower_whole
    anc_schur = (
        a22_anc
        + own_update
        - product(factor, lax.all_gather(anc_upper, ("row", "depth"), axis=0, tiled=True))
    )
    return (leaf_lower[None], leaf_upper[None], anc_lower, anc_upper, anc_schur)


def solution(mesh):
    in_specs = (
        P("depth", "row", "col"),
        P("depth", "row", "col"),
        P("depth", None, "col"),
        P("depth", "row", None),
        P("depth"),
        P("depth", "row"),
        P("depth", "col"),
        P(("row", "depth"), "col"),
        P(("row", "depth"), "col"),
        P(("row", "depth"), "col"),
        P(None, "col"),
        P(("row", "depth"), None),
    )
    out_specs = (
        P("depth", "row", "col"),
        P("depth", "row", "col"),
        P(("row", "depth"), "col"),
        P(("row", "depth"), "col"),
        P(("row", "depth"), "col"),
    )
    return jax.shard_map(shards, mesh=mesh, in_specs=in_specs, out_specs=out_specs, check_vma=False)
```

profile of v0, /device:TPU:0, one launch (start us, length us, event | category | flops | bytes accessed | tf_op | source)
XLA Modules:
  0.0 1554.8 jit_solution(6377144033500188488)
XLA Ops:
  7.2 0.7 all-gather.23.cloned.1.call-update
  8.0 0.7 all-gather.25.cloned.1.call-update
  8.7 0.7 all-gather.11.cloned.1.call-update
  10.1 106.2 %all-gather.23.cloned.1.call-done = f32[1,1024,2048]{2,1,0:T(8,128)} async-done(((f32[1,1024,1024]{2,1,0:T(8,128)}), f32[1,1024,2048]{2,1,0:T(8,128)}) %all-gather.23.cloned.1.call-update) | async-done | bytes 8388624 | tf_op jit(solution)/shard_map/all_gather | solution.py:78
  116.3 31.9 %fusion.15 = f32[1024,1024]{1,0:T(8,128)} fusion(f32[1,2048,1024]{2,1,0:T(8,128)} %param.14, f32[1,1024,2048]{2,1,0:T(8,128)} %all-gather.23.cloned.1.call-done, f32[1024]{0:T(1024)S(1)} %fusion.24), kind=kOutput, calls=%fused_computation.14 | convolution fusion | flops 25770852352 | bytes 20975616 | tf_op jit(solution)/shard_map/dot_general | solution.py:10
  148.3 256.4 %all-gather.25.cloned.1.call-done = f32[1,2048,2048]{2,1,0:T(8,128)} async-done(((f32[1,512,2048]{2,1,0:T(8,128)}), f32[1,2048,2048]{2,1,0:T(8,128)}) %all-gather.25.cloned.1.call-update) | async-done | bytes 16777232 | tf_op jit(solution)/shard_map/all_gather | solution.py:81
  404.6 32.8 %fusion.10 = f32[512,2048]{1,0:T(8,128)} fusion(f32[1,2048,2048]{2,1,0:T(8,128)} %all-gather.25.cloned.1.call-done, f32[1,512,2048]{2,1,0:T(8,128)} %param.15, f32[2048]{0:T(1024)S(1)} %fusion.20), kind=kOutput, calls=%fused_computation.13 | convolution fusion | flops 25770852352 | bytes 25174016 | tf_op jit(solution)/shard_map/dot_general | solution.py:10
  437.5 0.5 all-gather.13.cloned.1.call-update
  438.1 0.3 all-gather.19.cloned.1.call-start
  438.4 22.7 %all-gather.11.cloned.1.call-done = f32[512,2048]{1,0:T(8,128)} async-done(((f32[512,1024]{1,0:T(8,128)}), f32[512,2048]{1,0:T(8,128)}) %all-gather.11.cloned.1.call-update) | async-done | bytes 4194320 | tf_op jit(solution)/shard_map/all_gather | solution.py:44
  461.1 17.5 %fusion.28 = f32[512,1024]{1,0:T(8,128)} fusion(f32[512,2048]{1,0:T(8,128)} %all-gather.11.cloned.1.call-done, f32[2048,1024]{1,0:T(8,128)} %param.22), kind=kOutput, calls=%fused_computation.27 | convolution fusion | flops 12884901888 | bytes 14680064 | tf_op jit(solution)/shard_map/dot_general | solution.py:10
  478.7 88.4 %all-gather.15.cloned.1.call-done = f32[1024,2048]{1,0:T(8,128)} async-done(((f32[1024,1024]{1,0:T(8,128)}), f32[1024,2048]{1,0:T(8,128)}) %all-gather.15.cloned.1.call-update) | async-done | bytes 8388624 | tf_op jit(solution)/shard_map/all_gather | solution.py:86
  567.1 288.8 %all-gather.17.cloned.1.call-done = f32[2048,2048]{1,0:T(8,128)} async-done(((f32[512,2048]{1,0:T(8,128)}), f32[2048,2048]{1,0:T(8,128)}) %all-gather.17.cloned.1.call-update) | async-done | bytes 16777232 | tf_op jit(solution)/shard_map/all_gather | solution.py:83
  855.9 69.7 %subtract_bitcast_fusion = f32[128,8,16,128]{3,1,2,0:T(8,128)S(1)} fusion(f32[1024,2048]{1,0:T(8,128)} %all-gather.15.cloned.1.call-done, f32[2048,2048]{1,0:T(8,128)} %all-gather.17.cloned.1.call-done), kind=kOutput, calls=%fused_computation.11 | convolution fusion | flops 51541704704 | bytes 33554432 | tf_op jit(solution)/shard_map/dot_general | solution.py:10
  925.6 2.0 copy.21
  927.6 9.7 fusion.7
  937.4 21.8 %fusion.2 = f32[32,16,128,128]{3,0,2,1:T(8,128)} fusion(f32[16,128,16,128]{3,0,2,1:T(8,128)S(1)} %fusion.7, s32[16]{0:T(128)S(1)} %subtract_bitcast_fusion.2), kind=kOutput, calls=%fused_computation.3 | convolution fusion | flops 1610613248 | bytes 50331712 | tf_op jit(solution)/shard_map/axjy,jb->axby/dot_general | solution.py:37
  959.2 38.4 %copy.28 = f32[256,8,32,128]{3,1,2,0:T(8,128)} copy(f32[256,8,32,128]{3,2,1,0:T(8,128)} %bitcast.56) | data formatting | bytes 67108864
  997.6 26.0 %all-gather.13.cloned.1.call-done = f32[2048,4096]{1,0:T(8,128)} async-done(((f32[128,4096]{1,0:T(8,128)}), f32[2048,4096]{1,0:T(8,128)}) %all-gather.13.cloned.1.call-update) | async-done | bytes 33554448 | tf_op jit(solution)/shard_map/all_gather | solution.py:47
  1023.6 22.6 %fusion.29 = f32[128,4096]{1,0:T(8,128)} fusion(f32[128,2048]{1,0:T(8,128)S(1)} %copy-done, f32[2048,4096]{1,0:T(8,128)} %all-gather.13.cloned.1.call-done), kind=kOutput, calls=%fused_computation.28 | convolution fusion | flops 12884901888 | bytes 36700160 | tf_op jit(solution)/shard_map/dot_general | solution.py:10
  1046.2 36.3 %all-gather.19.cloned.1.call-done = f32[512,2048]{1,0:T(8,128)} async-done(((f32[512,1024]{1,0:T(8,128)}), f32[512,2048]{1,0:T(8,128)}) %all-gather.19.cloned.1.call-update) | async-done | bytes 4194320 | tf_op jit(solution)/shard_map/all_gather | solution.py:45
  1082.4 234.9 %reduce-scatter.2.cloned.1.call-done = f32[512,4096]{1,0:T(8,128)} async-done(((f32[2048,4096]{1,0:T(8,128)}), f32[512,4096]{1,0:T(8,128)}) %reduce-scatter.2.cloned.1.call-update) | async-done | bytes 8388624 | tf_op jit(solution)/shard_map/reduce_scatter | solution.py:14
  1317.4 170.3 %all-gather.21.cloned.1.call-done = f32[2048,4096]{1,0:T(8,128)} async-done(((f32[128,4096]{1,0:T(8,128)}), f32[2048,4096]{1,0:T(8,128)}) %all-gather.21.cloned.1.call-update) | async-done | bytes 33554448 | tf_op jit(solution)/shard_map/all_gather | solution.py:94
  1487.6 60.3 %add_subtract_fusion = f32[512,4096]{1,0:T(8,128)} fusion(f32[512,4096]{1,0:T(8,128)} %param.19, f32[512,4096]{1,0:T(8,128)} %reduce-scatter.2.cloned.1.call-done, f32[512,2048]{1,0:T(8,128)} %all-gather.19.cloned.1.call-done, f32[2048,4096]{1,0:T(8,128)} %all-gather.21.cloned.1.call-done), kind=kOutput, calls=%fused_computation.10 | convolution fusion | flops 51543801856 | bytes 62914560 | tf_op jit(solution)/shard_map/dot_general | solution.py:10
  (23 shorter events, 0.4 us)
Async XLA Ops:
  7.2 1016.4 %copy-start = (f32[128,2048]{1,0:T(8,128)S(1)}, f32[128,2048]{1,0:T(8,128)}, u32[]{:S(2)}) copy-start(f32[128,2048]{1,0:T(8,128)} %param.23) | copy-start | bytes 3145732
  7.2 109.1 %all-gather.23.cloned.1.call-start = ((), (), s32[]{:S(2)}) async-start(), calls=%async_computation.8 | async-start | bytes 12582912 | tf_op jit(solution)/shard_map/all_gather | solution.py:78
  7.9 396.7 %all-gather.25.cloned.1.call-start = ((), (), s32[]{:S(2)}) async-start(), calls=%async_computation.9 | async-start | bytes 20971520 | tf_op jit(solution)/shard_map/all_gather | solution.py:81
  8.7 452.5 %all-gather.11.cloned.1.call-start = ((), (), s32[]{:S(2)}) async-start(), calls=%async_computation.1 | async-start | bytes 6291456 | tf_op jit(solution)/shard_map/all_gather | solution.py:44
  9.4 557.7 %all-gather.15.cloned.1.call-start = ((), (), s32[]{:S(2)}) async-start(), calls=%async_computation.3 | async-start | bytes 12582912 | tf_op jit(solution)/shard_map/all_gather | solution.py:86
  148.2 707.7 %all-gather.17.cloned.1.call-start = ((), (), s32[]{:S(2)}) async-start(), calls=%async_computation.4 | async-start | bytes 20971520 | tf_op jit(solution)/shard_map/all_gather | solution.py:83
  148.2 290.1 %copy-start.1 = (s32[1,8]{1,0:T(1,128)S(1)}, s32[1,8]{1,0:T(1,128)}, u32[]{:S(2)}) copy-start(s32[1,8]{1,0:T(1,128)} %param.17) | copy-start | bytes 100
  148.2 290.1 %copy-start.2 = (s32[1,16]{1,0:T(1,128)S(1)}, s32[1,16]{1,0:T(1,128)}, u32[]{:S(2)}) copy-start(s32[1,16]{1,0:T(1,128)} %param.18) | copy-start | bytes 196
  437.5 586.1 %all-gather.13.cloned.1.call-start = ((), (), s32[]{:S(2)}) async-start(), calls=%async_computation.2 | async-start | bytes 35651584 | tf_op jit(solution)/shard_map/all_gather | solution.py:47
  438.1 644.4 %all-gather.19.cloned.1.call-start = ((), (), s32[]{:S(2)}) async-start(), calls=%async_computation.6 | async-start | bytes 6291456 | tf_op jit(solution)/shard_map/all_gather | solution.py:45
  478.7 838.7 %reduce-scatter.2.cloned.1.call-start = ((), (), s32[]{:S(2)}) async-start(), calls=%async_computation.5 | async-start | bytes 41943040 | tf_op jit(solution)/shard_map/reduce_scatter | solution.py:14
  997.5 490.1 %all-gather.21.cloned.1.call-start = ((), (), s32[]{:S(2)}) async-start(), calls=%async_computation.7 | async-start | bytes 35651584 | tf_op jit(solution)/shard_map/all_gather | solution.py:94
Sparse Core Ops, SparseCore 0:
  9.5 106.6 all-gather.22
  117.8 286.7 all-gather.24
  406.2 54.8 all-gather.10
  463.1 103.9 all-gather.14
  569.1 286.7 all-gather.16
  857.3 166.2 all-gather.12
  1025.7 56.6 all-gather.18
  1085.0 232.3 reduce-scatter.1
  1319.6 168.0 all-gather.20
where the time goes:
time: 1560 us; the launch traced here: 1550 us
  waiting for transfers between devices  1230 us (79%)
  matrix products  266 us (17%)
  local copies, waits for them, and re-layouts  40.4 us (3%)
    all_gather x1, waiting for transfers between devices, shards(): upper_whole = lax.all_gather(leaf_upper, 'row', axis=0, tiled=True)  289 us
    all_gather x1, waiting for transfers between devices, shards(): lax.all_gather(panel_top, 'row', axis=0, tiled=True)  256 us
    reduce_scatter x1, waiting for transfers between devices, reduce_depth(): return lax.psum_scatter(update, 'depth', scatter_dimension=0, tiled=True)  235 us
    dot_general x6, matrix products, product(): jnp.dot(left, right, precision=lax.Precision.HIGHEST, preferred_element_t...  235 us
    all_gather x1, waiting for transfers between devices, shards(): lax.all_gather(anc_upper, ('row', 'depth'), axis=0, tiled=True)  170 us
    all_gather x1, waiting for transfers between devices, shards(): lax.all_gather(panel_left, 'col', axis=1, tiled=True)  106 us
    all_gather x1, waiting for transfers between devices, shards(): lax.all_gather(leaf_lower, 'col', axis=1, tiled=True)  88.4 us
    unnamed x8, local copies, waits for them, and re-layouts  40.4 us
  transfers between devices with their start and end apart: 9, of which 9 were waited for; matrix products, arithmetic and copies ran while one was open for 16% of the time, Pallas kernels for 0%

commit v1 on v0

--- a/solution.py
+++ b/solution.py
@@ -1,9 +1,19 @@
+import functools
 import jax
 import jax.numpy as jnp
 from jax import lax
 from jax.sharding import PartitionSpec as P
 
 NB = 128
+
+
+def rings_proceed(local_values, group_axis, dim_at):
+    fresh = lax.all_gather(local_values, group_axis)
+    mid_arr = jnp.concatenate(fresh, dim_at)
+    return mid_arr
+
+
+note_the_plane = functools.partial(rings_proceed, group_axis="col", dim_at=1)
 
 
 def product(left, right):
@@ -83,7 +93,7 @@
     upper_whole = lax.all_gather(leaf_upper, "row", axis=0, tiled=True)
     factor = upper_whole
     schur = jnp.zeros((rows_here, cols_here), jnp.float32) - product(
-        lax.all_gather(leaf_lower, "col", axis=1, tiled=True), factor
+        note_the_plane(leaf_lower), factor
     )
     own_update = combine_depth(schur, row_map, col_map, a22_anc)
     anc_lower, lower_whole, anc_upper = anc_panels(a21_anc, a12_anc, uinv_anc, linv_anc)

time: 1560 us -> 1560 us (level)
  transfers between devices with their start and end apart: 9 -> 9, of which waited for: 9 -> 9; matrix products, arithmetic and copies ran while one was open for 16% -> 17% of each run, Pallas kernels for 0% -> 0%
where the time goes in v1:
time: 1560 us; the launch traced here: 1550 us
  waiting for transfers between devices  1220 us (78%)
  matrix products  269 us (17%)
  local copies, waits for them, and re-layouts  48.9 us (3%)
    all_gather x1, waiting for transfers between devices, shards(): upper_whole = lax.all_gather(leaf_upper, 'row', axis=0, tiled=True)  280 us
    all_gather x1, waiting for transfers between devices, shards(): lax.all_gather(panel_top, 'row', axis=0, tiled=True)  256 us
    dot_general x6, matrix products, product(): jnp.dot(left, right, precision=lax.Precision.HIGHEST, preferred_element_t...  238 us
    reduce_scatter x1, waiting for transfers between devices, reduce_depth(): return lax.psum_scatter(update, 'depth', scatter_dimension=0, tiled=True)  235 us
    all_gather x1, waiting for transfers between devices, shards(): lax.all_gather(anc_upper, ('row', 'depth'), axis=0, tiled=True)  170 us
    all_gather x1, waiting for transfers between devices, shards(): lax.all_gather(panel_left, 'col', axis=1, tiled=True)  106 us
    all_gather x1, waiting for transfers between devices, rings_proceed(): fresh = lax.all_gather(local_values, group_axis)  88.4 us
    unnamed x8, local copies, waits for them, and re-layouts  40.2 us
  transfers between devices with their start and end apart: 9, of which 9 were waited for; matrix products, arithmetic and copies ran while one was open for 17% of the time, Pallas kernels for 0%

profile of v1, /device:TPU:0, one launch (start us, length us, event | category | flops | bytes accessed | tf_op | source)
XLA Modules:
  0.0 1554.8 jit_solution(6031711031553715772)
XLA Ops:
  7.2 0.7 all-gather.22.cloned.1.call-update
  8.0 0.7 all-gather.24.cloned.1.call-update
  8.7 0.7 all-gather.12.cloned.1.call-update
  10.1 106.2 %all-gather.22.cloned.1.call-done = f32[1,1024,2048]{2,1,0:T(8,128)} async-done(((f32[1,1024,1024]{2,1,0:T(8,128)}), f32[1,1024,2048]{2,1,0:T(8,128)}) %all-gather.22.cloned.1.call-update) | async-done | bytes 8388624 | tf_op jit(solution)/shard_map/all_gather | solution.py:88
  116.3 31.9 %fusion.15 = f32[1024,1024]{1,0:T(8,128)} fusion(f32[1,2048,1024]{2,1,0:T(8,128)} %param.14, f32[1,1024,2048]{2,1,0:T(8,128)} %all-gather.22.cloned.1.call-done, f32[1024]{0:T(1024)S(1)} %fusion.24), kind=kOutput, calls=%fused_computation.14 | convolution fusion | flops 25770852352 | bytes 20975616 | tf_op jit(solution)/shard_map/dot_general | solution.py:20
  148.3 256.4 %all-gather.24.cloned.1.call-done = f32[1,2048,2048]{2,1,0:T(8,128)} async-done(((f32[1,512,2048]{2,1,0:T(8,128)}), f32[1,2048,2048]{2,1,0:T(8,128)}) %all-gather.24.cloned.1.call-update) | async-done | bytes 16777232 | tf_op jit(solution)/shard_map/all_gather | solution.py:91
  404.6 32.8 %fusion.10 = f32[512,2048]{1,0:T(8,128)} fusion(f32[1,2048,2048]{2,1,0:T(8,128)} %all-gather.24.cloned.1.call-done, f32[1,512,2048]{2,1,0:T(8,128)} %param.15, f32[2048]{0:T(1024)S(1)} %fusion.20), kind=kOutput, calls=%fused_computation.13 | convolution fusion | flops 25770852352 | bytes 25174016 | tf_op jit(solution)/shard_map/dot_general | solution.py:20
  437.5 0.5 all-gather.14.cloned.1.call-update
  438.4 22.7 %all-gather.12.cloned.1.call-done = f32[512,2048]{1,0:T(8,128)} async-done(((f32[512,1024]{1,0:T(8,128)}), f32[512,2048]{1,0:T(8,128)}) %all-gather.12.cloned.1.call-update) | async-done | bytes 4194320 | tf_op jit(solution)/shard_map/all_gather | solution.py:54
  461.1 17.5 %fusion.28 = f32[512,1024]{1,0:T(8,128)} fusion(f32[512,2048]{1,0:T(8,128)} %all-gather.12.cloned.1.call-done, f32[2048,1024]{1,0:T(8,128)} %param.22), kind=kOutput, calls=%fused_computation.27 | convolution fusion | flops 12884901888 | bytes 14680064 | tf_op jit(solution)/shard_map/dot_general | solution.py:20
  478.7 88.4 %all-gather.26.cloned.1.call-done = f32[2048,1024]{1,0:T(8,128)} async-done(((f32[1024,1024]{1,0:T(8,128)}), f32[2048,1024]{1,0:T(8,128)}) %all-gather.26.cloned.1.call-update) | async-done | bytes 8388624 | tf_op jit(solution)/shard_map/all_gather | solution.py:11
  567.1 8.7 copy.17
  575.8 280.1 %all-gather.16.cloned.1.call-done = f32[2048,2048]{1,0:T(8,128)} async-done(((f32[512,2048]{1,0:T(8,128)}), f32[2048,2048]{1,0:T(8,128)}) %all-gather.16.cloned.1.call-update) | async-done | bytes 16777232 | tf_op jit(solution)/shard_map/all_gather | solution.py:93
  855.9 72.9 %subtract_bitcast_fusion = f32[128,8,16,128]{3,1,2,0:T(8,128)S(1)} fusion(f32[1024,2048]{0,1:T(8,128)} %bitcast.63, f32[2048,2048]{1,0:T(8,128)} %all-gather.16.cloned.1.call-done), kind=kOutput, calls=%fused_computation.11 | convolution fusion | flops 51541704704 | bytes 33554432 | tf_op jit(solution)/shard_map/dot_general | solution.py:20
  928.8 2.0 copy.22
  930.8 9.7 fusion.7
  940.5 21.8 %fusion.2 = f32[32,16,128,128]{3,0,2,1:T(8,128)} fusion(f32[16,128,16,128]{3,0,2,1:T(8,128)S(1)} %fusion.7, s32[16]{0:T(128)S(1)} %subtract_bitcast_fusion.2), kind=kOutput, calls=%fused_computation.3 | convolution fusion | flops 1610613248 | bytes 50331712 | tf_op jit(solution)/shard_map/axjy,jb->axby/dot_general | solution.py:47
  962.3 38.2 %copy.29 = f32[256,8,32,128]{3,1,2,0:T(8,128)} copy(f32[256,8,32,128]{3,2,1,0:T(8,128)} %bitcast.60) | data formatting | bytes 67108864
  1000.6 23.0 %all-gather.14.cloned.1.call-done = f32[2048,4096]{1,0:T(8,128)} async-done(((f32[128,4096]{1,0:T(8,128)}), f32[2048,4096]{1,0:T(8,128)}) %all-gather.14.cloned.1.call-update) | async-done | bytes 33554448 | tf_op jit(solution)/shard_map/all_gather | solution.py:57
  1023.6 22.6 %fusion.29 = f32[128,4096]{1,0:T(8,128)} fusion(f32[128,2048]{1,0:T(8,128)S(1)} %copy-done, f32[2048,4096]{1,0:T(8,128)} %all-gather.14.cloned.1.call-done), kind=kOutput, calls=%fused_computation.28 | convolution fusion | flops 12884901888 | bytes 36700160 | tf_op jit(solution)/shard_map/dot_general | solution.py:20
  1046.2 36.3 %all-gather.18.cloned.1.call-done = f32[512,2048]{1,0:T(8,128)} async-done(((f32[512,1024]{1,0:T(8,128)}), f32[512,2048]{1,0:T(8,128)}) %all-gather.18.cloned.1.call-update) | async-done | bytes 4194320 | tf_op jit(solution)/shard_map/all_gather | solution.py:55
  1082.5 234.9 %reduce-scatter.2.cloned.1.call-done = f32[512,4096]{1,0:T(8,128)} async-done(((f32[2048,4096]{1,0:T(8,128)}), f32[512,4096]{1,0:T(8,128)}) %reduce-scatter.2.cloned.1.call-update) | async-done | bytes 8388624 | tf_op jit(solution)/shard_map/reduce_scatter | solution.py:24
  1317.4 170.3 %all-gather.20.cloned.1.call-done = f32[2048,4096]{1,0:T(8,128)} async-done(((f32[128,4096]{1,0:T(8,128)}), f32[2048,4096]{1,0:T(8,128)}) %all-gather.20.cloned.1.call-update) | async-done | bytes 33554448 | tf_op jit(solution)/shard_map/all_gather | solution.py:104
  1487.6 60.3 %add_subtract_fusion = f32[512,4096]{1,0:T(8,128)} fusion(f32[512,4096]{1,0:T(8,128)} %param.19, f32[512,4096]{1,0:T(8,128)} %reduce-scatter.2.cloned.1.call-done, f32[512,2048]{1,0:T(8,128)} %all-gather.18.cloned.1.call-done, f32[2048,4096]{1,0:T(8,128)} %all-gather.20.cloned.1.call-done), kind=kOutput, calls=%fused_computation.10 | convolution fusion | flops 51543801856 | bytes 62914560 | tf_op jit(solution)/shard_map/dot_general | solution.py:20
  (24 shorter events, 0.7 us)
Async XLA Ops:
  7.2 1016.4 %copy-start = (f32[128,2048]{1,0:T(8,128)S(1)}, f32[128,2048]{1,0:T(8,128)}, u32[]{:S(2)}) copy-start(f32[128,2048]{1,0:T(8,128)} %param.23) | copy-start | bytes 3145732
  7.2 109.1 %all-gather.22.cloned.1.call-start = ((), (), s32[]{:S(2)}) async-start(), calls=%async_computation.7 | async-start | bytes 12582912 | tf_op jit(solution)/shard_map/all_gather | solution.py:88
  7.9 396.7 %all-gather.24.cloned.1.call-start = ((), (), s32[]{:S(2)}) async-start(), calls=%async_computation.8 | async-start | bytes 20971520 | tf_op jit(solution)/shard_map/all_gather | solution.py:91
  8.7 452.5 %all-gather.12.cloned.1.call-start = ((), (), s32[]{:S(2)}) async-start(), calls=%async_computation.1 | async-start | bytes 6291456 | tf_op jit(solution)/shard_map/all_gather | solution.py:54
  9.4 557.7 %all-gather.26.cloned.1.call-start = ((), (), s32[]{:S(2)}) async-start(), calls=%async_computation.9 | async-start | bytes 12582912 | tf_op jit(solution)/shard_map/all_gather | solution.py:11
  148.2 707.7 %all-gather.16.cloned.1.call-start = ((), (), s32[]{:S(2)}) async-start(), calls=%async_computation.3 | async-start | bytes 20971520 | tf_op jit(solution)/shard_map/all_gather | solution.py:93
  148.2 290.1 %copy-start.1 = (s32[1,8]{1,0:T(1,128)S(1)}, s32[1,8]{1,0:T(1,128)}, u32[]{:S(2)}) copy-start(s32[1,8]{1,0:T(1,128)} %param.17) | copy-start | bytes 100
  148.2 290.1 %copy-start.2 = (s32[1,16]{1,0:T(1,128)S(1)}, s32[1,16]{1,0:T(1,128)}, u32[]{:S(2)}) copy-start(s32[1,16]{1,0:T(1,128)} %param.18) | copy-start | bytes 196
  437.5 586.1 %all-gather.14.cloned.1.call-start = ((), (), s32[]{:S(2)}) async-start(), calls=%async_computation.2 | async-start | bytes 35651584 | tf_op jit(solution)/shard_map/all_gather | solution.py:57
  438.1 644.4 %all-gather.18.cloned.1.call-start = ((), (), s32[]{:S(2)}) async-start(), calls=%async_computation.5 | async-start | bytes 6291456 | tf_op jit(solution)/shard_map/all_gather | solution.py:55
  478.7 838.7 %reduce-scatter.2.cloned.1.call-start = ((), (), s32[]{:S(2)}) async-start(), calls=%async_computation.4 | async-start | bytes 41943040 | tf_op jit(solution)/shard_map/reduce_scatter | solution.py:24
  1000.5 487.1 %all-gather.20.cloned.1.call-start = ((), (), s32[]{:S(2)}) async-start(), calls=%async_computation.6 | async-start | bytes 35651584 | tf_op jit(solution)/shard_map/all_gather | solution.py:104
Sparse Core Ops, SparseCore 0:
  9.5 106.6 all-gather.21
  117.8 286.7 all-gather.23
  406.2 54.8 all-gather.11
  463.1 103.9 all-gather.25
  569.1 286.7 all-gather.15
  857.3 166.2 all-gather.13
  1025.7 56.6 all-gather.17
  1085.0 232.3 reduce-scatter.1
  1319.6 168.0 all-gather.19
